TPU v7x, 32 devices: a whole 2x2x4 slice. The times are simulated.
32 devices in a mesh: dp: 4 (over y, x), vocab: 8 (over z, core).
Axes of the slice: x: 2, y: 2, z: 4, core: 2. Of those that a mesh axis runs over, the one named last changes fastest.
Arguments:
- hidden: bfloat16 [256, 4096], P('dp'), may hold values from -0.75 to 0.75
- head_weight: bfloat16 [4096, 128256], P(None, ('dp', 'vocab')), may hold values from -0.75 to 0.75
- target_ids: int32 [256], P('dp'), may hold values from 0 to 128255
- loss_mask: int32 [256], P('dp'), may hold values from 0 to 1, as said below
- doc_ids: int32 [256], P('dp'), may hold values from 0 to 31, as said below
- loss_scale: float32 [], replicated, may hold values from 512 to 2048
Outputs:
- mean_loss: float32 [], replicated
- head_grad: bfloat16 [4096, 128256], P(None, ('dp', 'vocab'))
- hidden_grad: bfloat16 [256, 4096], P(None, ('dp', 'vocab'))
Inputs may be any that keep to these rules, and one draw needn't show every extreme that they name: loss_mask is 0 or 1; among the 64 positions of each data group (aligned blocks of 64 positions) at most 32 have loss_mask 1, and exactly 32 in one of them; the last position of each data group has loss_mask 1. doc_ids starts at 0 and never falls; from one position to the next it grows by 0 or 1; its last value is 31.
All inputs are finite; a program needn't handle non-finite values.
Results may differ from a plain program's by a relative error of at most 0.0017.
Values may be sent and summed in bfloat16 or wider, within the bound.
A program may use at most 128 MiB of HBM per device.

v0:
```python
import jax
import jax.numpy as jnp
from jax import lax
from jax.sharding import PartitionSpec as P

VALID_MOST = 32


def shifted(value, axis, steps):
    count = lax.axis_size(axis)
    leading, last = max(0, -steps), min(count, count - steps)
    return lax.ppermute(value, axis, [(source, source + steps) for source in range(leading, last)])


def on_device(hidden, head_weight, target_ids, loss_mask, doc_ids, loss_scale):
    tok_dev = hidden.shape[0]
    model_width = hidden.shape[1]
    block_cols = head_weight.shape[1]
    col_base = lax.axis_index(("dp", "vocab")) * block_cols
    group_offset = lax.axis_index("dp") * tok_dev
    next_first = shifted(doc_ids[:1] + 1, "dp", -1)
    following = jnp.concatenate([doc_ids[1:] + 1, next_first])
    valid_rows = loss_mask * (following == doc_ids + 1).astype(jnp.int32)
    ranked = jnp.argsort(1 - valid_rows, stable=True)[:VALID_MOST].astype(jnp.int32)
    local_rows = hidden[ranked]
    local_targets = target_ids[ranked]
    local_valid = valid_rows[ranked]
    local_positions = ranked + group_offset
    rows_all = lax.all_gather(local_rows, "dp", axis=0, tiled=True)
    targets_all, valid_all, positions = (
        lax.all_gather(local_targets, "dp", axis=0, tiled=True),
        lax.all_gather(local_valid, "dp", axis=0, tiled=True),
        lax.all_gather(local_positions, "dp", axis=0, tiled=True),
    )
    logits = jnp.dot(rows_all, head_weight, preferred_element_type=jnp.float32)
    local_max = jnp.max(logits, axis=1)
    shifted_ids = targets_all - col_base
    inside = (shifted_ids >= 0) & (shifted_ids < block_cols)
    picked = jnp.take_along_axis(logits, jnp.clip(shifted_ids, 0, block_cols - 1)[:, None], axis=1)[
        :, 0
    ]
    target_part = jnp.where(inside, picked, 0.0)
    row_max = lax.pmax(local_max, ("dp", "vocab"))
    local_sum = jnp.sum(jnp.exp(logits - row_max[:, None]), axis=1)
    row_total, target_logit = lax.psum((local_sum, target_part), ("dp", "vocab"))
    log_total = row_max + jnp.log(row_total)
    weight_rows = valid_all.astype(jnp.float32)
    valid_count = jnp.sum(weight_rows)
    mean_loss = jnp.sum((log_total - target_logit) * weight_rows) / valid_count
    prob_rows = jnp.exp(logits - log_total[:, None])
    onehot = (jnp.arange(block_cols, dtype=jnp.int32)[None, :] == shifted_ids[:, None]).astype(
        jnp.float32
    )
    grad_scale = weight_rows * (loss_scale / valid_count)
    grad_logits = ((prob_rows - onehot) * grad_scale[:, None]).astype(jnp.bfloat16)
    head_grad = lax.dot_general(
        rows_all, grad_logits, (((0,), (0,)), ((), ())), preferred_element_type=jnp.float32
    ).astype(jnp.bfloat16)

    def hidden_term():
        weight_part = lax.slice_in_dim(
            head_weight, 0, own_cols * lax.axis_size(("dp", "vocab")), axis=0
        )
        return lax.dot_general(
            weight_part, grad_logits, (((1,), (1,)), ((), ())), preferred_element_type=jnp.float32
        )

    own_cols = model_width // lax.axis_size(("dp", "vocab"))
    hidden_terms = lax.psum_scatter(hidden_term(), ("dp", "vocab"), scatter_dimension=0, tiled=True)
    total_rows = tok_dev * lax.axis_size("dp")
    placed = jnp.zeros((total_rows, own_cols), jnp.float32).at[positions].set(hidden_terms.T)
    hidden_grad = placed.astype(jnp.bfloat16)
    return (mean_loss, head_grad, hidden_grad)


def solution(mesh):
    return jax.shard_map(
        on_device,
        mesh=mesh,
        in_specs=(P("dp", None), P(None, ("dp", "vocab")), P("dp"), P("dp"), P("dp"), P()),
        out_specs=(P(), P(None, ("dp", "vocab")), P(None, ("dp", "vocab"))),
        check_vma=False,
    )
```

profile of v0, /device:TPU:0, one launch (start us, length us, event | category | flops | bytes accessed | tf_op | source)
XLA Modules:
  0.0 309.2 jit_solution(16839350995757339751)
XLA Ops:
  7.9 1.3 collective-permute-start
  9.2 0.7 slice_add_fusion
  10.0 1.2 dynamic-slice
  11.9 2.5 collective-permute-done
  14.3 1.4 broadcast_subtract_fusion.1
  15.8 2.0 sort.17
  17.9 1.4 gather_fusion
  20.1 0.7 gather_fusion.2
  20.8 0.7 gather_fusion.1
  21.5 0.2 dynamic-update-slice.1
  21.7 0.2 dynamic-update-slice
  21.9 9.7 %all-reduce.3 = (s32[128]{0:T(128)S(1)}, s32[128]{0:T(128)S(1)}, s32[128]{0:T(128)S(1)}) all-reduce(s32[128]{0:T(128)S(1)} %dynamic-update-slice.1, s32[128]{0:T(128)S(1)} %dynamic-update-slice, s32[128]{0:T(128)S(1)} %get-tuple-element.17), channel_id=4, replica_groups=mesh['dp'=4,'vocab'=8] {'dp'}, use_global_device_ids=true, to_apply=%add.1 | all-reduce | flops 384 | bytes 3072
  31.7 16.8 %all-gather.5.cloned.1.call-done = bf16[128,4096]{1,0:T(8,128)(2,1)} async-done(((bf16[32,4096]{1,0:T(8,128)(2,1)}), bf16[128,4096]{1,0:T(8,128)(2,1)}) %all-gather.5.cloned.1.call-update) | async-done | bytes 1048592 | tf_op jit(solution)/shard_map/all_gather | solution.py:29
  48.5 14.2 %fusion.4 = (f32[128]{0:T(128)S(1)}, f32[128,4008]{0,1:T(8,128)S(1)}) fusion(bf16[128,4096]{1,0:T(8,128)(2,1)} %all-gather.5.cloned.1.call-done, bf16[4096,4008]{0,1:T(8,128)(2,1)} %param.7), kind=kOutput, calls=%fused_computation.31 | convolution fusion | flops 4203205632 | bytes 35934720 | tf_op jit(solution)/shard_map/dot_general | solution.py:35
  62.8 39.4 %pmax.7 = f32[128]{0:T(128)S(1)} all-reduce(f32[128]{0:T(128)S(1)} %get-tuple-element.19), channel_id=1, replica_groups=mesh['dp'=4,'vocab'=8] {'dp','vocab'}, use_global_device_ids=true, to_apply=%region_2.3 | all-reduce | flops 128 | bytes 1024 | tf_op jit(solution)/shard_map/pmax | solution.py:43
  102.1 1.3 gather_fusion.3
  103.4 0.6 exponential_reduce_fusion
  104.0 41.1 %all-reduce.4 = (f32[128]{0:T(128)S(1)}, f32[128]{0:T(128)S(1)}) all-reduce(f32[128]{0:T(128)S(1)} %exponential_reduce_fusion, f32[128]{0:T(128)S(1)} %and_select_fusion.1), channel_id=1, replica_groups=mesh['dp'=4,'vocab'=8] {'dp','vocab'}, use_global_device_ids=true, to_apply=%region_4.5 | all-reduce | flops 256 | bytes 2048 | tf_op jit(solution)/shard_map/psum | solution.py:45
  145.1 0.6 convert_reduce_fusion
  146.5 14.6 %convolution_bitcast_fusion = f32[4096,128]{0,1:T(8,128)} fusion(bf16[4096,4008]{0,1:T(8,128)(2,1)} %param.7, f32[128,4008]{0,1:T(8,128)S(1)} %get-tuple-element.20, f32[128]{0:T(128)S(1)} %convert_multiply_fusion, s32[128]{0:T(128)S(1)} %get-tuple-element.14, f32[128]{0:T(128)S(1)} %get-tuple-element.12), kind=kOutput, calls=%fused_computation.6 | convolution fusion | flops 4205770752 | bytes 36984320 | tf_op jit(solution)/shard_map/dot_general | solution.py:64
  162.4 15.8 %convolution_convert_fusion = bf16[4096,4008]{0,1:T(8,128)(2,1)} fusion(bf16[128,4096]{1,0:T(8,128)(2,1)} %all-gather.5.cloned.1.call-done, f32[128,4008]{0,1:T(8,128)S(1)} %get-tuple-element.20, f32[128]{0:T(128)S(1)} %convert_multiply_fusion, s32[128]{0:T(128)S(1)} %get-tuple-element.14, f32[128]{0:T(128)S(1)} %get-tuple-element.12), kind=kOutput, calls=%fused_computation.5 | convolution fusion | flops 4222187520 | bytes 35935744 | tf_op jit(solution)/shard_map/dot_general | solution.py:56
  178.2 121.2 %reduce-scatter.2.cloned.1.call-done = f32[128,128]{0,1:T(8,128)} async-done(((f32[4096,128]{0,1:T(8,128)}), f32[128,128]{0,1:T(8,128)}) %reduce-scatter.2.cloned.1.call-update) | async-done | bytes 65552 | tf_op jit(solution)/shard_map/reduce_scatter | solution.py:69
  299.3 1.2 scatter_custom_fusion
  300.6 0.6 convert_element_type.20
  (23 shorter events, 0.3 us)
Async XLA Ops:
  7.2 10.8 %copy-start = (bf16[64,4096]{1,0:T(8,128)(2,1)S(1)}, bf16[64,4096]{1,0:T(8,128)(2,1)}, u32[]{:S(2)}) copy-start(bf16[64,4096]{1,0:T(8,128)(2,1)} %param.6) | copy-start | bytes 1572868
  7.2 13.6 %copy-start.2 = (s32[64]{0:T(128)S(1)}, s32[64]{0:T(128)}, u32[]{:S(2)}) copy-start(s32[64]{0:T(128)} %param.8) | copy-start | bytes 772
  7.2 41.3 %all-gather.5.cloned.1.call-start = ((), (), s32[]{:S(2)}) async-start(), calls=%async_computation.2 | async-start | bytes 1310720 | tf_op jit(solution)/shard_map/all_gather | solution.py:29
  7.9 6.4 %collective-permute-start = (s32[1]{0:T(128)}, s32[1]{0:T(128)}, u32[]{:S(2)}, u32[]{:S(2)}) collective-permute-start(s32[1]{0:T(128)} %add.50), channel_id=1, source_target_pairs={{8,0},{16,8},{24,16},{9,1},{17,9},{25,17},{10,2},{18,10},{26,18},{... | collective-permute-start | bytes 20 | tf_op jit(solution)/shard_map/ppermute | solution.py:12
  19.4 280.0 %reduce-scatter.2.cloned.1.call-start = ((), (), s32[]{:S(2)}) async-start(), calls=%async_computation.1 | async-start | bytes 2162688 | tf_op jit(solution)/shard_map/reduce_scatter | solution.py:69
  162.4 138.8 %copy-start.1 = (bf16[64,4096]{1,0:T(8,128)(2,1)S(1)}, bf16[64,4096]{1,0:T(8,128)(2,1)}, u32[]{:S(2)}) copy-start(bf16[64,4096]{1,0:T(8,128)(2,1)} %param.6) | copy-start | bytes 1572868
Sparse Core Ops, SparseCore 0:
  19.5 28.9 all-gather.4
  161.2 138.1 reduce-scatter.1
where the time goes:
time: 310 us; the launch traced here: 309 us
  waiting for transfers between devices  140 us (45%)
  blocking collectives  90.3 us (29%)
  matrix products  44.6 us (14%)
  between operations  19.3 us (6%)
  local copies, waits for them, and re-layouts  7.03 us (2%)
  other arithmetic  6.14 us (2%)
    reduce_scatter x1, waiting for transfers between devices, on_device(): lax.psum_scatter(hidden_term(), ('dp', 'vocab'), scatter_dimension=0, til...  121 us
    psum x1, blocking collectives, on_device(): lax.psum((local_sum, target_part), ('dp', 'vocab'))  41.1 us
    pmax x1, blocking collectives, on_device(): row_max = lax.pmax(local_max, ('dp', 'vocab'))  39.4 us
    all_gather x1, waiting for transfers between devices, on_device(): rows_all = lax.all_gather(local_rows, 'dp', axis=0, tiled=True)  16.8 us
    dot_general x1, matrix products, on_device(): lax.dot_general(rows_all, grad_logits, (((0,), (0,)), ((), ())), preferre...  15.8 us
    dot_general x1, matrix products, hidden_term(): lax.dot_general(weight_part, grad_logits, (((1,), (1,)), ((), ())), prefe...  14.6 us
    dot_general x1, matrix products, on_device(): logits = jnp.dot(rows_all, head_weight, preferred_element_type=jnp.float32)  14.2 us
    unnamed x1, blocking collectives  9.73 us
  transfers between devices with their start and end apart: 3, of which 3 were waited for; matrix products, arithmetic and copies ran while one was open for 6% of the time, Pallas kernels for 0%

commit v1 on v0

v1 whole, which is shorter than its diff:
```python
import functools

import jax
import jax.numpy as jnp
from jax import lax
from jax.experimental import pallas as pl
from jax.experimental.pallas import tpu as pltpu
from jax.sharding import PartitionSpec as P

VALID_MOST = 32
MESH = pl.DeviceIdType.MESH
VMEM = pl.BlockSpec(memory_space=pltpu.VMEM)
SMEM = pl.BlockSpec(memory_space=pltpu.SMEM)
F32 = jnp.float32
BF16 = jnp.bfloat16


def remote(src, dst, send_sem, recv_sem, where):
    return pltpu.make_async_remote_copy(
        src_ref=src, dst_ref=dst, send_sem=send_sem, recv_sem=recv_sem, device_id=where, device_id_type=MESH
    )


def greet(where):
    pl.semaphore_signal(pltpu.get_barrier_semaphore(), inc=1, device_id=where, device_id_type=MESH)


def gather_kernel(n_dp, hidden, targets, mask, docs, rows, meta_out, meta, merged, row_s, row_r, fwd_s, fwd_r, meta_s, meta_r):
    d, v = lax.axis_index("dp"), lax.axis_index("vocab")
    core = lax.rem(v, 2)
    partner = (d, v + 1 - 2 * core)
    peers = [lax.rem(d + k, n_dp) for k in range(n_dp)]
    for k in range(1, n_dp):
        greet((peers[k], v))
    greet(partner)

    tok = hidden.shape[0]
    half = VALID_MOST // 2
    u = lax.broadcasted_iota(jnp.int32, (tok, tok), 0)
    t = lax.broadcasted_iota(jnp.int32, (tok, tok), 1)
    mask_f = jnp.broadcast_to(mask[...].astype(F32), (8, tok))
    docs_f = jnp.broadcast_to(docs[...].astype(F32), (8, tok))
    upto = jnp.where(u <= t, 1.0, 0.0).astype(BF16)
    after = jnp.where(u == t + 1, 1.0, 0.0).astype(BF16)
    rank = jnp.dot(mask_f.astype(BF16), upto, preferred_element_type=F32)[0:1] - 1.0
    following = jnp.dot(docs_f.astype(BF16), after, preferred_element_type=F32)[0:1]
    mask_f, docs_f = mask_f[0:1], docs_f[0:1]
    slot = lax.broadcasted_iota(jnp.int32, (VALID_MOST, tok), 0).astype(F32)
    chosen = jnp.where(slot == rank, 1.0, 0.0) * mask_f
    picked = jnp.dot(chosen.astype(BF16), hidden[...], preferred_element_type=F32).astype(BF16)
    rows[d, 0] = picked[:half]
    rows[d, 1] = picked[half:]
    place = lax.broadcasted_iota(jnp.int32, (1, tok), 1)
    inner = jnp.where(place < tok - 1, 1.0, 0.0)
    same = jnp.where(following == docs_f, 1.0, 0.0) * inner

    def column(values):
        return jnp.sum(chosen * values, axis=1, keepdims=True)

    fields = [
        column(targets[...].astype(F32)),
        column(same),
        column((place + d * tok).astype(F32)),
        jnp.broadcast_to(docs_f[:, 0:1], (VALID_MOST, 1)),
        column(1.0 - inner),
        jnp.broadcast_to(docs_f[:, tok - 1 : tok], (VALID_MOST, 1)),
    ]
    lane = lax.broadcasted_iota(jnp.int32, (VALID_MOST, 128), 1)
    packed = jnp.zeros((VALID_MOST, 128), F32)
    for number, field in enumerate(fields):
        packed = jnp.where(lane == number, field, packed)
    meta[d] = packed

    pl.semaphore_wait(pltpu.get_barrier_semaphore(), n_dp)
    sends = []
    for k in range(1, n_dp):
        sends.append(remote(rows.at[d, core], rows.at[d, core], row_s.at[k], row_r.at[k], (peers[k], v)))
        sends.append(remote(meta.at[d], meta.at[d], meta_s.at[k], meta_r.at[k], (peers[k], v)))
    for copy in sends:
        copy.start()
    forwards = []
    for k in range(1, n_dp):
        source = lax.rem(d + n_dp - k, n_dp)
        block = rows.at[source, core]
        remote(block, block, row_s.at[k], row_r.at[k], (peers[k], v)).wait_recv()
        copy = remote(block, block, fwd_s.at[k], fwd_r.at[k], partner)
        copy.start()
        forwards.append(copy)
    for k in range(1, n_dp):
        source = lax.rem(d + n_dp - k, n_dp)
        remote(meta.at[source], meta.at[source], meta_s.at[k], meta_r.at[k], (peers[k], v)).wait_recv()
    for group in range(n_dp):
        block = meta[group]
        valid = block[:, 1:2]
        if group < n_dp - 1:
            first = meta[group + 1][:, 3:4]
            valid = valid + block[:, 4:5] * jnp.where(block[:, 5:6] == first, 1.0, 0.0)
        merged[group * VALID_MOST : (group + 1) * VALID_MOST] = jnp.where(lane == 1, valid, block)
    meta_out[...] = merged[...].T[:8]
    for k in range(1, n_dp):
        source = lax.rem(d + n_dp - k, n_dp)
        other = rows.at[source, 1 - core]
        remote(other, other, fwd_s.at[k], fwd_r.at[k], partner).wait_recv()
    for copy in sends + forwards:
        copy.wait_send()


def gather_rows(n_dp, hidden, targets, mask, docs):
    width = hidden.shape[1]
    dma = pltpu.SemaphoreType.DMA((n_dp,))
    total = n_dp * VALID_MOST
    return pl.pallas_call(
        functools.partial(gather_kernel, n_dp),
        out_shape=(
            jax.ShapeDtypeStruct((n_dp, 2, VALID_MOST // 2, width), BF16),
            jax.ShapeDtypeStruct((8, total), F32),
        ),
        in_specs=[VMEM] * 4,
        out_specs=(VMEM, VMEM),
        scratch_shapes=[pltpu.VMEM((n_dp, VALID_MOST, 128), F32), pltpu.VMEM((total, 128), F32)] + [dma] * 6,
        compiler_params=pltpu.CompilerParams(collective_id=0, has_side_effects=True),
    )(hidden, targets[None], mask[None], docs[None])


def stats_kernel(n_dp, n_v, top, total, hit, meta, scale, out, slots, send, recv):
    d, v = lax.axis_index("dp"), lax.axis_index("vocab")
    me = d * n_v + v
    count = n_dp * n_v

    def device(k):
        index = lax.rem(me + k, count)
        return (index // n_v, lax.rem(index, n_v))

    def hello(k, carry):
        greet(device(k))
        return carry

    lax.fori_loop(1, count, hello, 0)
    line = lax.broadcasted_iota(jnp.int32, slots.shape[1:], 0)
    slots[me] = jnp.where(line == 0, top[...], jnp.where(line == 1, total[...], hit[...]))
    pl.semaphore_wait(pltpu.get_barrier_semaphore(), count - 1)

    def push(k, carry):
        remote(slots.at[me], slots.at[me], send.at[k], recv.at[k], device(k)).start()
        return carry

    lax.fori_loop(1, count, push, 0)

    def arrive(k, carry):
        source = slots.at[lax.rem(me + count - k, count)]
        copy = remote(source, source, send.at[k], recv.at[k], device(k))
        copy.wait_recv()
        copy.wait_send()
        return carry

    lax.fori_loop(1, count, arrive, 0)
    every = slots[...]
    row_max = jnp.max(every, axis=0)[0:1]
    row_total = jnp.sum(every[:, 1:2, :] * jnp.exp(every[:, 0:1, :] - row_max), axis=0)
    target_logit = jnp.sum(every, axis=0)[2:3]
    log_total = row_max + jnp.log(row_total)
    weight = meta[1:2, :]
    valid_count = jnp.sum(weight, axis=1, keepdims=True)
    mean_loss = jnp.sum((log_total - target_logit) * weight, axis=1, keepdims=True) / valid_count
    grad_scale = weight * (scale[0, 0] / valid_count)
    out[...] = jnp.where(line == 0, log_total, jnp.where(line == 1, grad_scale, mean_loss))


def share_stats(n_dp, n_v, top, total, hit, meta, scale):
    count = n_dp * n_v
    rows = top.shape[0]
    dma = pltpu.SemaphoreType.DMA((count,))
    return pl.pallas_call(
        functools.partial(stats_kernel, n_dp, n_v),
        out_shape=jax.ShapeDtypeStruct((8, rows), F32),
        in_specs=[VMEM] * 4 + [SMEM],
        out_specs=VMEM,
        scratch_shapes=[pltpu.VMEM((count, 8, rows), F32), dma, dma],
        compiler_params=pltpu.CompilerParams(collective_id=1, has_side_effects=True),
    )(top[None], total[None], hit[None], meta, scale.reshape(1, 1))


def scatter_kernel(n_dp, n_z, term, meta, out, got1, sum1, got2, sum2, got3, s1, r1, s2, r2, s3, r3):
    d, v = lax.axis_index("dp"), lax.axis_index("vocab")
    z, core = v // 2, lax.rem(v, 2)
    partner = (d, v + 1 - 2 * core)
    peers = [lax.rem(d + k, n_dp) for k in range(n_dp)]
    greet(partner)
    for k in range(1, n_dp):
        greet((peers[k], v))

    def along(step):
        return lax.rem(z + step, n_z)

    def hello(step, carry):
        greet((d, 2 * along(step) + core))
        return carry

    lax.fori_loop(1, n_z, hello, 0)
    pl.semaphore_wait(pltpu.get_barrier_semaphore(), n_dp + n_z - 1)

    order = list(range(1, n_dp)) + [0]

    def first(k):
        return remote(term.at[peers[k], :, 1 - core], got1.at[peers[k]], s1.at[k], r1.at[k], partner)

    def second(k, step):
        at = along(step)
        return remote(sum1.at[peers[k], at], got2.at[k, at], s2.at[k, step], r2.at[k, step], (peers[k], v))

    def third(step):
        at = along(step)
        return remote(sum2.at[at], got3.at[step], s3.at[step], r3.at[step], (d, 2 * at + core))

    for k in order:
        first(k).start()
    for k in order:
        first(k).wait_recv()

        def combine(step, carry, k=k):
            at = along(step)
            sum1[peers[k], at] = term[peers[k], at, core] + got1[peers[k], at]
            if k:
                second(k, step).start()
            return carry

        lax.fori_loop(1, n_z + 1, combine, 0)

    def merge(step, carry):
        at = along(step)
        value = sum1[d, at]
        for k in range(1, n_dp):
            second(k, step).wait_recv()
            value = value + got2[k, at]
        sum2[at] = value
        return carry

    def forward(step, carry):
        merge(step, 0)
        third(step).start()
        return carry

    lax.fori_loop(1, n_z, forward, 0)
    merge(n_z, 0)

    def finish(step, value):
        third(step).wait_recv()
        return value + got3[step]

    value = lax.fori_loop(1, n_z, finish, sum2[z])
    tokens = out.shape[0]
    spot = lax.broadcasted_iota(jnp.int32, (tokens, value.shape[1]), 0).astype(F32)
    onehot = jnp.where(spot == meta[2:3, :], 1.0, 0.0).astype(BF16)
    high = value.astype(BF16)
    rest = value - high.astype(F32)
    middle = rest.astype(BF16)
    low = (rest - middle.astype(F32)).astype(BF16)
    placed = jnp.zeros(out.shape, F32)
    for part in (low, middle, high):
        placed = placed + lax.dot_general(onehot, part, (((1,), (1,)), ((), ())), preferred_element_type=F32)
    out[...] = placed.astype(BF16)

    for k in order:
        first(k).wait_send()

    def drain2(step, carry):
        for k in range(1, n_dp):
            second(k, step).wait_send()
        return carry

    def drain3(step, carry):
        third(step).wait_send()
        return carry

    lax.fori_loop(1, n_z + 1, drain2, 0)
    lax.fori_loop(1, n_z, drain3, 0)


def scatter_terms(n_dp, n_v, term, meta, tokens):
    n_z = n_v // 2
    own, rows = term.shape[0] // (n_dp * n_v), term.shape[1]
    dma = pltpu.SemaphoreType.DMA
    return pl.pallas_call(
        functools.partial(scatter_kernel, n_dp, n_z),
        out_shape=jax.ShapeDtypeStruct((tokens, own), BF16),
        in_specs=[VMEM] * 2,
        out_specs=VMEM,
        scratch_shapes=[
            pltpu.VMEM((n_dp, n_z, own, rows), F32),
            pltpu.VMEM((n_dp, n_z, own, rows), F32),
            pltpu.VMEM((n_dp, n_z, own, rows), F32),
            pltpu.VMEM((n_z, own, rows), F32),
            pltpu.VMEM((n_z, own, rows), F32),
            dma((n_dp,)),
            dma((n_dp,)),
            dma((n_dp, n_z + 1)),
            dma((n_dp, n_z + 1)),
            dma((n_z,)),
            dma((n_z,)),
        ],
        compiler_params=pltpu.CompilerParams(collective_id=2, has_side_effects=True),
    )(term.reshape(n_dp, n_z, 2, own, rows), meta)


def on_device(n_dp, n_v, hidden, head_weight, target_ids, loss_mask, doc_ids, loss_scale):
    width, block_cols = head_weight.shape
    rows, meta = gather_rows(n_dp, hidden, target_ids, loss_mask, doc_ids)
    rows_all = rows.reshape(n_dp * VALID_MOST, width)
    col_base = lax.axis_index(("dp", "vocab")) * block_cols
    shifted_ids = meta[0].astype(jnp.int32) - col_base
    logits = jnp.dot(rows_all, head_weight, preferred_element_type=F32)
    local_max = jnp.max(logits, axis=1)
    onehot = jnp.arange(block_cols, dtype=jnp.int32)[None, :] == shifted_ids[:, None]
    target_part = jnp.sum(jnp.where(onehot, logits, 0.0), axis=1)
    local_sum = jnp.sum(jnp.exp(logits - local_max[:, None]), axis=1)
    stats = share_stats(n_dp, n_v, local_max, local_sum, target_part, meta, loss_scale)
    log_total, grad_scale, mean_loss = stats[0], stats[1], stats[2, 0]
    prob_rows = jnp.exp(logits - log_total[:, None])
    grad_logits = ((prob_rows - onehot.astype(F32)) * grad_scale[:, None]).astype(BF16)
    term = lax.dot_general(head_weight, grad_logits, (((1,), (1,)), ((), ())), preferred_element_type=F32)
    hidden_grad = scatter_terms(n_dp, n_v, term, meta, hidden.shape[0] * n_dp)
    head_grad = lax.dot_general(rows_all, grad_logits, (((0,), (0,)), ((), ())), preferred_element_type=F32).astype(BF16)
    return (mean_loss, head_grad, hidden_grad)


def solution(mesh):
    return jax.shard_map(
        functools.partial(on_device, mesh.shape["dp"], mesh.shape["vocab"]),
        mesh=mesh,
        in_specs=(P("dp", None), P(None, ("dp", "vocab")), P("dp"), P("dp"), P("dp"), P()),
        out_specs=(P(), P(None, ("dp", "vocab")), P(None, ("dp", "vocab"))),
        check_vma=False,
    )
```

time: 310 us -> 102 us (0.33)
  waiting for transfers between devices: 140 us -> 0 us
  blocking collectives: 90.3 us -> 0 us
  Pallas kernels: 0 us -> 50.2 us
  between operations: 19.3 us -> 1.35 us
  other arithmetic: 6.14 us -> 1.76 us
    reduce_scatter x1 -> x0, waiting for transfers between devices: 121 us -> none  [on_device(): lax.psum_scatter(hidden_term(), ('dp', 'vocab'), scatter_dimension=0, til...]
    pallas_call x0 -> x3, Pallas kernels: none -> 50.2 us  [the longest x1 24 us: scatter_terms(): pl.pallas_call(functools.partial(scatter_kernel, n_dp, n_z), out_shape=ja...]
    psum x1 -> x0, blocking collectives: 41.1 us -> none  [on_device(): lax.psum((local_sum, target_part), ('dp', 'vocab'))]
    pmax x1 -> x0, blocking collectives: 39.4 us -> none  [on_device(): row_max = lax.pmax(local_max, ('dp', 'vocab'))]
    all_gather x1 -> x0, waiting for transfers between devices: 16.8 us -> none  [on_device(): rows_all = lax.all_gather(local_rows, 'dp', axis=0, tiled=True)]
    unnamed x1 -> x0, blocking collectives: 9.73 us -> none
    gather x4 -> x0, local copies, waits for them, and re-layouts: 4.1 us -> none  [the longest x1 1.41 us: on_device(): local_rows = hidden[ranked]]
  transfers between devices with their start and end apart: 3 -> 0, of which waited for: 3 -> 0; matrix products, arithmetic and copies ran while one was open for 6% -> 0% of each run, Pallas kernels for 0% -> 0%
where the time goes in v1:
time: 102 us
  Pallas kernels  50.2 us (49%)
  matrix products  43.2 us (42%)
  local copies, waits for them, and re-layouts  5.54 us (5%)
  other arithmetic  1.76 us (2%)
  between operations  1.35 us (1%)
    pallas_call x1, Pallas kernels, scatter_terms(): pl.pallas_call(functools.partial(scatter_kernel, n_dp, n_z), out_shape=ja...  24 us
    dot_general x1, matrix products, on_device(): lax.dot_general(rows_all, grad_logits, (((0,), (0,)), ((), ())), preferre...  14.5 us
    dot_general x1, matrix products, on_device(): lax.dot_general(head_weight, grad_logits, (((1,), (1,)), ((), ())), prefe...  14.5 us
    pallas_call x1, Pallas kernels, gather_rows(): pl.pallas_call(functools.partial(gather_kernel, n_dp), out_shape=(jax.Sha...  14.3 us
    dot_general x1, matrix products, on_device(): logits = jnp.dot(rows_all, head_weight, preferred_element_type=F32)  14.3 us
    pallas_call x1, Pallas kernels, share_stats(): pl.pallas_call(functools.partial(stats_kernel, n_dp, n_v), out_shape=jax....  11.9 us
    dot_general x1, local copies, waits for them, and re-layouts, on_device(): lax.dot_general(head_weight, grad_logits, (((1,), (1,)), ((), ())), prefe...  2.94 us

profile of v1, /device:TPU:0, one launch (start us, length us, event | category | flops | bytes accessed | tf_op | source)
XLA Modules:
  0.0 102.0 jit_solution(16341009590756445489)
XLA Ops:
  1.3 14.3 %shard_map.85 = (bf16[4,2,16,4096]{3,2,1,0:T(8,128)(2,1)}, f32[8,128]{1,0:T(8,128)}) custom-call(bf16[64,4096]{1,0:T(8,128)(2,1)} %hidden.1, s32[1,64]{1,0:T(1,128)} %bitcast.29, s32[1,64]{1,0:T(1,128)} %bitcast.30, s32[1,64]{1,0:T(1,128)} %bitcast.31), custom_call_target="tpu_custom_call" | custom-call | tf_op jit(solution)/shard_map/pallas_call | solution.py:112
  15.6 0.7 subtract_bitcast_fusion
  16.3 14.3 %fusion = (f32[128]{0:T(128)S(1)}, f32[128,4008]{0,1:T(8,128)S(1)}) fusion(bf16[128,4096]{1,0:T(8,128)(2,1)} %bitcast.24, bf16[4096,4008]{0,1:T(8,128)(2,1)} %param.7), kind=kOutput, calls=%fused_computation.9 | convolution fusion | flops 4203205632 | bytes 35934720 | tf_op jit(solution)/shard_map/dot_general | solution.py:311
  30.6 0.0 copy-start.2
  30.6 1.1 %select_reduce_fusion = (f32[128]{0:T(128)}, f32[128]{0:T(128)}) fusion(f32[128,4008]{0,1:T(8,128)S(1)} %get-tuple-element.12, s32[128]{0:T(128)S(1)} %subtract_bitcast_fusion, f32[128]{0:T(128)S(1)} %get-tuple-element.11), kind=kLoop, calls=%fused_computation.3 | loop fusion | flops 2564864 | bytes 2054144 | tf_op jit(solution)/shard_map/reduce_sum | solution.py:314
  31.7 0.0 copy-done.2
  31.7 11.9 %shard_map.86 = f32[8,128]{1,0:T(8,128)} custom-call(f32[1,128]{1,0:T(1,128)} %bitcast.26, f32[1,128]{1,0:T(1,128)} %bitcast.28, f32[1,128]{1,0:T(1,128)} %bitcast.27, f32[8,128]{1,0:T(8,128)} %get-tuple-element.6.meta, f32[1,1]{1,0:T(1,128)} %bitcast.22.scale), custom_call_target="tpu_custom_call" | custom-call | tf_op jit(solution)/shard_map/pallas_call | solution.py:173
  43.5 1.2 %slice.13 = f32[1,1]{1,0:T(1,128)} slice(f32[8,128]{1,0:T(8,128)} %shard_map.86), slice={[2:3], [0:1]} | slice | bytes 8 | tf_op jit(solution)/shard_map/slice | solution.py:317
  44.7 0.8 slice_bitcast_fusion.1
  45.5 14.5 %convolution_bitcast_fusion = f32[4096,128]{0,1:T(8,128)} fusion(bf16[4096,4008]{0,1:T(8,128)(2,1)} %param.7, f32[128,4008]{0,1:T(8,128)S(1)} %get-tuple-element.12, f32[128]{0:T(128)S(1)} %get-tuple-element.10, f32[128]{0:T(128)S(1)} %get-tuple-element.9, s32[128]{0:T(128)S(1)} %subtract_bitcast_fusion), kind=kOutput, calls=%fused_computation.1 | convolution fusion | flops 4205770752 | bytes 36984320 | tf_op jit(solution)/shard_map/dot_general | solution.py:320
  59.9 2.9 %copy.9 = f32[4096,128]{1,0:T(8,128)} copy(f32[4096,128]{0,1:T(8,128)} %convolution_bitcast_fusion) | data formatting | bytes 4194304 | tf_op jit(solution)/shard_map/dot_general | solution.py:320
  62.9 0.0 copy-start
  62.9 24.0 %shard_map.87 = bf16[256,128]{1,0:T(8,128)(2,1)} custom-call(f32[4,4,2,128,128]{4,3,2,1,0:T(8,128)} %bitcast.23, f32[8,128]{1,0:T(8,128)} %get-tuple-element.6.meta), custom_call_target="tpu_custom_call" | custom-call | tf_op jit(solution)/shard_map/pallas_call | solution.py:283
  86.9 0.0 copy-done
  86.9 0.0 copy-start.1
  86.9 14.5 %convolution_convert_fusion = bf16[4096,4008]{0,1:T(8,128)(2,1)} fusion(bf16[128,4096]{1,0:T(8,128)(2,1)S(1)} %bitcast.25, f32[128,4008]{0,1:T(8,128)S(1)} %get-tuple-element.12, f32[128]{0:T(128)S(1)} %get-tuple-element.10, f32[128]{0:T(128)S(1)} %get-tuple-element.9, s32[128]{0:T(128)S(1)} %subtract_bitcast_fusion), kind=kOutput, calls=%fused_computation | convolution fusion | flops 4222187520 | bytes 35935744 | tf_op jit(solution)/shard_map/dot_general | solution.py:322
  101.4 0.0 copy-done.1
  101.4 0.6 copy.12
Async XLA Ops:
  30.6 1.1 %copy-start.2 = (f32[128]{0:T(128)}, f32[128]{0:T(128)S(1)}, u32[]{:S(2)}) copy-start(f32[128]{0:T(128)S(1)} %get-tuple-element.11) | copy-start | bytes 1540
  62.9 24.0 %copy-start = (bf16[4,2,16,4096]{3,2,1,0:T(8,128)(2,1)S(1)}, bf16[4,2,16,4096]{3,2,1,0:T(8,128)(2,1)}, u32[]{:S(2)}) copy-start(bf16[4,2,16,4096]{3,2,1,0:T(8,128)(2,1)} %get-tuple-element.5) | copy-start | bytes 3145732
  86.9 14.5 %copy-start.1 = (bf16[256,128]{1,0:T(8,128)(2,1)S(1)}, bf16[256,128]{1,0:T(8,128)(2,1)}, u32[]{:S(2)}) copy-start(bf16[256,128]{1,0:T(8,128)(2,1)} %shard_map.87) | copy-start | bytes 196612

commit v2 on v1

--- a/solution.py
+++ b/solution.py
@@ -180,11 +180,25 @@
     )(top[None], total[None], hit[None], meta, scale.reshape(1, 1))
 
 
-def scatter_kernel(n_dp, n_z, term, meta, out, got1, sum1, got2, sum2, got3, s1, r1, s2, r2, s3, r3):
+def scatter_kernel(n_dp, n_z, weight, grads_t, meta, out, grads, panels, fetched, term, got1, sum1, got2, sum2, got3, s1, r1, s2, r2, s3, r3):
     d, v = lax.axis_index("dp"), lax.axis_index("vocab")
     z, core = v // 2, lax.rem(v, 2)
     partner = (d, v + 1 - 2 * core)
     peers = [lax.rem(d + k, n_dp) for k in range(n_dp)]
+    order = list(range(1, n_dp)) + [0]
+    slots, _, chunk = panels.shape
+    own = term.shape[3]
+    parts = weight.shape[1] // n_dp // chunk
+    steps = [(k, part) for k in order for part in range(parts)]
+
+    def fetch(number):
+        k, part = steps[number]
+        start = pl.multiple_of((peers[k] * parts + part) * chunk, chunk)
+        slot = number % slots
+        return pltpu.make_async_copy(weight.at[:, pl.ds(start, chunk)], panels.at[slot], fetched.at[slot])
+
+    for number in range(slots):
+        fetch(number).start()
     greet(partner)
     for k in range(1, n_dp):
         greet((peers[k], v))
@@ -197,9 +211,6 @@
         return carry
 
     lax.fori_loop(1, n_z, hello, 0)
-    pl.semaphore_wait(pltpu.get_barrier_semaphore(), n_dp + n_z - 1)
-
-    order = list(range(1, n_dp)) + [0]
 
     def first(k):
         return remote(term.at[peers[k], :, 1 - core], got1.at[peers[k]], s1.at[k], r1.at[k], partner)
@@ -212,12 +223,30 @@
         at = along(step)
         return remote(sum2.at[at], got3.at[step], s3.at[step], r3.at[step], (d, 2 * at + core))
 
-    for k in order:
-        first(k).start()
-    for k in order:
+    grads[...] = grads_t[...].T
+
+    def multiply(number):
+        k, part = steps[number]
+        slot = number % slots
+        fetch(number).wait()
+        tile = min(256, chunk)
+
+        def column(j, carry):
+            panel = panels[slot, :, pl.ds(pl.multiple_of(j * tile, tile), tile)]
+            block = jnp.dot(grads[...], panel, preferred_element_type=F32).T
+            deep = tile // (2 * own)
+            base = part * (chunk // (2 * own)) + j * deep
+            term[peers[k], pl.ds(base, deep)] = block.reshape(deep, 2, own, block.shape[1])
+            return carry
+
+        lax.fori_loop(0, chunk // tile, column, 0)
+        if number + slots < len(steps):
+            fetch(number + slots).start()
+
+    def join(k):
         first(k).wait_recv()
 
-        def combine(step, carry, k=k):
+        def combine(step, carry):
             at = along(step)
             sum1[peers[k], at] = term[peers[k], at, core] + got1[peers[k], at]
             if k:
@@ -225,6 +254,16 @@
             return carry
 
         lax.fori_loop(1, n_z + 1, combine, 0)
+
+    for number, (k, part) in enumerate(steps):
+        multiply(number)
+        if number == 0:
+            pl.semaphore_wait(pltpu.get_barrier_semaphore(), n_dp + n_z - 1)
+        if part == parts - 1:
+            first(k).start()
+        if part == 0 and number:
+            join(steps[number - 1][0])
+    join(order[-1])
 
     def merge(step, carry):
         at = along(step)
@@ -276,16 +315,22 @@
     lax.fori_loop(1, n_z, drain3, 0)
 
 
-def scatter_terms(n_dp, n_v, term, meta, tokens):
+def scatter_terms(n_dp, n_v, weight, grads, meta, tokens):
     n_z = n_v // 2
-    own, rows = term.shape[0] // (n_dp * n_v), term.shape[1]
+    columns, width = weight.shape
+    own, rows = width // (n_dp * n_v), grads.shape[1]
+    chunk = width // n_dp // 2
     dma = pltpu.SemaphoreType.DMA
     return pl.pallas_call(
         functools.partial(scatter_kernel, n_dp, n_z),
         out_shape=jax.ShapeDtypeStruct((tokens, own), BF16),
-        in_specs=[VMEM] * 2,
+        in_specs=[pl.BlockSpec(memory_space=pl.ANY), VMEM, VMEM],
         out_specs=VMEM,
         scratch_shapes=[
+            pltpu.VMEM((rows, columns), BF16),
+            pltpu.VMEM((4, columns, chunk), BF16),
+            dma((4,)),
+            pltpu.VMEM((n_dp, n_z, 2, own, rows), F32),
             pltpu.VMEM((n_dp, n_z, own, rows), F32),
             pltpu.VMEM((n_dp, n_z, own, rows), F32),
             pltpu.VMEM((n_dp, n_z, own, rows), F32),
@@ -298,8 +343,8 @@
             dma((n_z,)),
             dma((n_z,)),
         ],
-        compiler_params=pltpu.CompilerParams(collective_id=2, has_side_effects=True),
-    )(term.reshape(n_dp, n_z, 2, own, rows), meta)
+        compiler_params=pltpu.CompilerParams(collective_id=2, has_side_effects=True, vmem_limit_bytes=40 * 1024 * 1024),
+    )(weight, grads, meta)
 
 
 def on_device(n_dp, n_v, hidden, head_weight, target_ids, loss_mask, doc_ids, loss_scale):
@@ -317,8 +362,7 @@
     log_total, grad_scale, mean_loss = stats[0], stats[1], stats[2, 0]
     prob_rows = jnp.exp(logits - log_total[:, None])
     grad_logits = ((prob_rows - onehot.astype(F32)) * grad_scale[:, None]).astype(BF16)
-    term = lax.dot_general(head_weight, grad_logits, (((1,), (1,)), ((), ())), preferred_element_type=F32)
-    hidden_grad = scatter_terms(n_dp, n_v, term, meta, hidden.shape[0] * n_dp)
+    hidden_grad = scatter_terms(n_dp, n_v, head_weight.T, grad_logits.T, meta, hidden.shape[0] * n_dp)
     head_grad = lax.dot_general(rows_all, grad_logits, (((0,), (0,)), ((), ())), preferred_element_type=F32).astype(BF16)
     return (mean_loss, head_grad, hidden_grad)
 

time: 102 us -> 86.6 us (0.85)
  matrix products: 43.2 us -> 28.7 us
  local copies, waits for them, and re-layouts: 5.54 us -> 2.66 us
    dot_general x1 -> x0, matrix products: 14.5 us -> none  [on_device(): lax.dot_general(head_weight, grad_logits, (((1,), (1,)), ((), ())), prefe...]
    dot_general x1 -> x0, local copies, waits for them, and re-layouts: 2.94 us -> none  [on_device(): lax.dot_general(head_weight, grad_logits, (((1,), (1,)), ((), ())), prefe...]
where the time goes in v2:
time: 86.6 us; the launch traced here: 86.2 us
  Pallas kernels  51 us (59%)
  matrix products  28.7 us (33%)
  local copies, waits for them, and re-layouts  2.66 us (3%)
  other arithmetic  2.44 us (3%)
  between operations  1.35 us (2%)
    pallas_call x1, Pallas kernels, scatter_terms(): pl.pallas_call(functools.partial(scatter_kernel, n_dp, n_z), out_shape=ja...  24.8 us
    dot_general x1, matrix products, on_device(): lax.dot_general(rows_all, grad_logits, (((0,), (0,)), ((), ())), preferre...  14.5 us
    pallas_call x1, Pallas kernels, gather_rows(): pl.pallas_call(functools.partial(gather_kernel, n_dp), out_shape=(jax.Sha...  14.3 us
    dot_general x1, matrix products, on_device(): logits = jnp.dot(rows_all, head_weight, preferred_element_type=F32)  14.3 us
    pallas_call x1, Pallas kernels, share_stats(): pl.pallas_call(functools.partial(stats_kernel, n_dp, n_v), out_shape=jax....  11.9 us

profile of v2, /device:TPU:0, one launch (start us, length us, event | category | flops | bytes accessed | tf_op | source)
XLA Modules:
  0.0 86.2 jit_solution(9245280791491906530)
XLA Ops:
  0.6 14.3 %shard_map.85 = (bf16[4,2,16,4096]{3,2,1,0:T(8,128)(2,1)}, f32[8,128]{1,0:T(8,128)}) custom-call(bf16[64,4096]{1,0:T(8,128)(2,1)} %hidden.1, s32[1,64]{1,0:T(1,128)} %bitcast.32, s32[1,64]{1,0:T(1,128)} %bitcast.33, s32[1,64]{1,0:T(1,128)} %bitcast.34), custom_call_target="tpu_custom_call" | custom-call | tf_op jit(solution)/shard_map/pallas_call | solution.py:112
  15.0 14.3 %fusion.5 = (f32[128]{0:T(128)S(1)}, f32[128,4008]{0,1:T(8,128)S(1)}) fusion(bf16[128,4096]{1,0:T(8,128)(2,1)} %bitcast.27, bf16[4096,4008]{0,1:T(8,128)(2,1)} %param.7), kind=kOutput, calls=%fused_computation.16 | convolution fusion | flops 4203205632 | bytes 35934720 | tf_op jit(solution)/shard_map/dot_general | solution.py:356
  29.3 0.0 copy-start.2
  29.3 0.0 copy-start.1
  29.3 0.8 subtract_bitcast_fusion
  30.1 1.1 %select_reduce_fusion = (f32[128]{0:T(128)}, f32[128]{0:T(128)}) fusion(f32[128,4008]{0,1:T(8,128)S(1)} %get-tuple-element.12, s32[128]{0:T(128)S(1)} %subtract_bitcast_fusion, f32[128]{0:T(128)S(1)} %get-tuple-element.11), kind=kLoop, calls=%fused_computation.7 | loop fusion | flops 2564864 | bytes 2054144 | tf_op jit(solution)/shard_map/reduce_sum | solution.py:359
  31.8 0.0 copy-done.2
  31.8 11.9 %shard_map.86 = f32[8,128]{1,0:T(8,128)} custom-call(f32[1,128]{1,0:T(1,128)} %bitcast.29, f32[1,128]{1,0:T(1,128)} %bitcast.31, f32[1,128]{1,0:T(1,128)} %bitcast.30, f32[8,128]{1,0:T(8,128)} %get-tuple-element.6.meta, f32[1,1]{1,0:T(1,128)} %bitcast.25.scale), custom_call_target="tpu_custom_call" | custom-call | tf_op jit(solution)/shard_map/pallas_call | solution.py:173
  43.7 1.2 %slice.13 = f32[1,1]{1,0:T(1,128)} slice(f32[8,128]{1,0:T(8,128)} %shard_map.86), slice={[2:3], [0:1]} | slice | bytes 8 | tf_op jit(solution)/shard_map/slice | solution.py:362
  44.9 0.8 slice_bitcast_fusion.1
  45.6 0.0 copy-done.1
  45.6 14.5 %convolution_convert_fusion = bf16[4096,4008]{0,1:T(8,128)(2,1)} fusion(bf16[128,4096]{1,0:T(8,128)(2,1)S(1)} %bitcast.28, f32[128,4008]{0,1:T(8,128)S(1)} %get-tuple-element.12, f32[128]{0:T(128)S(1)} %get-tuple-element.10, f32[128]{0:T(128)S(1)} %get-tuple-element.9, s32[128]{0:T(128)S(1)} %subtract_bitcast_fusion), kind=kOutput, calls=%fused_computation | convolution fusion | flops 4222187520 | bytes 35935744 | tf_op jit(solution)/shard_map/dot_general | solution.py:366
  60.1 0.0 copy-start
  60.1 0.6 fusion.1.grads_t
  60.7 0.1 copy-done
  60.8 24.8 %shard_map.87 = bf16[256,128]{1,0:T(8,128)(2,1)S(1)} custom-call(bf16[4008,4096]{1,0:T(8,128)(2,1)} %bitcast.26, bf16[4008,128]{1,0:T(8,128)(2,1)S(1)} %fusion.1.grads_t, f32[8,128]{1,0:T(8,128)S(1)} %copy-done), custom_call_target="tpu_custom_call" | custom-call | tf_op jit(solution)/shard_map/pallas_call | solution.py:324
  85.6 0.6 copy.11
Async XLA Ops:
  29.3 2.5 %copy-start.2 = (f32[128]{0:T(128)}, f32[128]{0:T(128)S(1)}, u32[]{:S(2)}) copy-start(f32[128]{0:T(128)S(1)} %get-tuple-element.11) | copy-start | bytes 1540
  29.3 16.3 %copy-start.1 = (bf16[4,2,16,4096]{3,2,1,0:T(8,128)(2,1)S(1)}, bf16[4,2,16,4096]{3,2,1,0:T(8,128)(2,1)}, u32[]{:S(2)}) copy-start(bf16[4,2,16,4096]{3,2,1,0:T(8,128)(2,1)} %get-tuple-element.5) | copy-start | bytes 3145732
  60.1 0.7 copy-start
